TPU v7x, 128 devices: a whole 4x4x4 slice. The times are simulated.
128 devices in a mesh: act: 4 (over y), virt: 32 (over x, z, core).
Axes of the slice: x: 4, y: 4, z: 4, core: 2. Of those that a mesh axis runs over, the one named last changes fastest.
Arguments:
- amplitudes: bfloat16 [400, 640, 640], P('act', 'virt'), may hold values from -6 to 6
- virtual_fock_block: bfloat16 [640, 640], replicated, may hold values from -1 to 3.1, as said below
- metric: bfloat16 [400, 400], replicated, may hold values from -3.5 to 3.5, as said below
- active_block: bfloat16 [400, 400], replicated, may hold values from -0.3125 to 0.3125
Outputs:
- residual_vec: bfloat16 [400, 640, 640], P('act', 'virt')
- rayleigh: float32 [], replicated
- res_norm: float32 [], replicated
Inputs may be any that keep to these rules, and one draw needn't show every extreme that they name: `virtual_fock_block`: symmetric. `metric`: symmetric positive definite.
All inputs are finite; a program needn't handle non-finite values.
Results may differ from a plain program's by a relative error of at most 0.0099.
Values may be sent and summed in bfloat16 or wider, within the bound.
No kernel may reach another device: no remote copies, remote signals or barrier semaphores. Data moves between devices by JAX's collectives and lax.ppermute only.
A program may use at most 128 MiB of HBM per device.

v0:
```python
import functools

import jax
import jax.numpy as jnp
from jax import lax
from jax.experimental import pallas as pl
from jax.experimental.pallas import tpu as pltpu
from jax.sharding import PartitionSpec as P

BF = jnp.bfloat16
F32 = jnp.float32
ALL = ("act", "virt")
LANES = 128
USED = 125
VMEM_LIMIT = 60 * 1024 * 1024
NT_DIMS = (((1,), (1,)), ((), ()))
TN_DIMS = (((0,), (0,)), ((), ()))


def onehot(shape, row_base, column_base, row_end, column_end):
    rows = lax.broadcasted_iota(jnp.int32, shape, 0)
    columns = lax.broadcasted_iota(jnp.int32, shape, 1)
    same = (rows + row_base) == (columns + column_base)
    keep = same & (rows < row_end) & (columns < column_end)
    return jnp.where(keep, 1.0, 0.0).astype(BF)


def touching(pairs, items):
    chunks = pairs * items // USED
    return [
        [i for i in range(items) if i * pairs < (k + 1) * USED and (i + 1) * pairs > k * USED]
        for k in range(chunks)
    ]


def pack_kernel(pitch, x_ref, out_ref, scratch):
    rows, pairs, width = x_ref.shape
    items = width // LANES
    table = touching(pairs, items)
    chunks = len(table)
    sel = {
        (k, i): onehot((pairs, LANES), i * pairs, k * USED, pairs, USED)
        for k in range(chunks)
        for i in table[k]
    }
    for a in range(rows):
        for k in range(chunks):
            total = None
            for i in table[k]:
                part = lax.dot_general(
                    x_ref[a, :, i * LANES : (i + 1) * LANES], sel[k, i], TN_DIMS, preferred_element_type=F32
                )
                total = part if total is None else total + part
            scratch[pl.ds(k * rows + a, LANES, stride=pitch), :] = total
    used = chunks * rows
    for d in range(LANES):
        out_ref[d] = scratch[d * pitch : d * pitch + used, :].astype(BF)


def pack(x):
    rows, pairs, width = x.shape
    used = pairs * (width // LANES) // USED * rows
    pitch = used + 8
    return pl.pallas_call(
        functools.partial(pack_kernel, pitch),
        out_shape=jax.ShapeDtypeStruct((LANES, used, LANES), BF),
        in_specs=[pl.BlockSpec(memory_space=pltpu.VMEM)],
        out_specs=pl.BlockSpec(memory_space=pltpu.VMEM),
        scratch_shapes=[pltpu.VMEM((LANES * pitch, LANES), F32)],
        compiler_params=pltpu.CompilerParams(vmem_limit_bytes=VMEM_LIMIT),
    )(x)


def mid_kernel(
    acts, rows, pairs, items, r_ref, f_ref, m_ref, h_ref, out_ref, flat, unsel, padded, u_ref, w_ref, s_ref
):
    count = r_ref.shape[0] // acts
    wide = count * rows
    chunks = pairs * items // USED
    used = chunks * rows
    for k in range(chunks):
        for i in range(items):
            unsel[k * LANES : (k + 1) * LANES, i * LANES : (i + 1) * LANES] = onehot(
                (LANES, LANES), k * USED, i * pairs, USED, pairs
            )
    for j in range(acts):
        padded[j * LANES : (j + 1) * LANES, :] = onehot((LANES, acts * pairs), j * pairs, 0, pairs, acts * pairs)

    def spread(matrix):
        half = lax.dot_general(padded[...], matrix, NT_DIMS, preferred_element_type=F32).astype(BF)
        return lax.dot_general(half, padded[...], NT_DIMS, preferred_element_type=F32).astype(BF)

    m_wide = spread(m_ref[...])
    h_wide = spread(h_ref[...])

    def arrive(j, carry):
        for v in range(count):
            block = r_ref[j * count + v].astype(F32)
            for k in range(chunks):
                flat[v * rows : (v + 1) * rows, k * LANES : (k + 1) * LANES] = block[k * rows : (k + 1) * rows]
        u_ref[j] = jnp.dot(flat[...].astype(BF), unsel[...], preferred_element_type=F32).astype(BF)
        return carry

    lax.fori_loop(0, acts, arrive, 0)
    for i in range(items):
        cols = slice(i * LANES, (i + 1) * LANES)
        u = jnp.concatenate([u_ref[j, :, cols] for j in range(acts)], axis=1)
        w = jnp.dot(u, m_wide, preferred_element_type=F32).astype(BF)
        s = jnp.dot(f_ref[...], w, preferred_element_type=F32)
        s = (s + jnp.dot(u, h_wide, preferred_element_type=F32)).astype(BF)
        for j in range(acts):
            w_ref[j, :, cols] = w[:, j * LANES : (j + 1) * LANES]
            s_ref[j, :, cols] = s[:, j * LANES : (j + 1) * LANES]

    def leave(j, carry):
        for n, source in enumerate((w_ref, s_ref)):
            flat[...] = lax.dot_general(source[j], unsel[...], NT_DIMS, preferred_element_type=F32)
            for v in range(count):
                block = jnp.concatenate(
                    [
                        flat[v * rows : (v + 1) * rows, k * LANES : (k + 1) * LANES]
                        for k in range(chunks)
                    ],
                    axis=0,
                )
                out_ref[j * count + v, n * used : (n + 1) * used, :] = block.astype(BF)
        return carry

    lax.fori_loop(0, acts, leave, 0)


def middle(received, fock, metric, active, acts, rows, pairs, items):
    count = received.shape[0] // acts
    wide = count * rows
    chunks = pairs * items // USED
    vmem = pl.BlockSpec(memory_space=pltpu.VMEM)
    return pl.pallas_call(
        functools.partial(mid_kernel, acts, rows, pairs, items),
        out_shape=jax.ShapeDtypeStruct((LANES, 2 * chunks * rows, LANES), BF),
        in_specs=[vmem] * 4,
        out_specs=vmem,
        scratch_shapes=[
            pltpu.VMEM((wide, chunks * LANES), F32),
            pltpu.VMEM((chunks * LANES, items * LANES), BF),
            pltpu.VMEM((acts * LANES, acts * pairs), BF),
            pltpu.VMEM((acts, wide, items * LANES), BF),
            pltpu.VMEM((acts, wide, items * LANES), BF),
            pltpu.VMEM((acts, wide, items * LANES), BF),
        ],
        compiler_params=pltpu.CompilerParams(vmem_limit_bytes=VMEM_LIMIT),
    )(received, fock, metric, active)


def last_kernel(pitch, r_ref, x_ref, f_ref, sigma_ref, w_ref, sums_ref, scratch, w_all, s_all):
    rows, pairs, width = x_ref.shape
    items = width // LANES
    chunks = pairs * items // USED
    used = chunks * rows
    table = touching(pairs, items)
    tall = w_all.shape[0] // rows
    for d in range(LANES):
        scratch[d * pitch : d * pitch + 2 * used, :] = r_ref[d].astype(F32)
    sel = {
        (k, i): onehot((tall, LANES), i * pairs, k * USED, pairs, USED)
        for k in range(chunks)
        for i in table[k]
    }
    for a in range(rows):
        for n, target in enumerate((w_all, s_all)):
            got = [
                scratch[pl.ds(n * used + k * rows + a, LANES, stride=pitch), :].astype(BF)
                for k in range(chunks)
            ]
            for i in range(items):
                total = None
                for k in range(chunks):
                    if i in table[k]:
                        part = lax.dot_general(sel[k, i], got[k], NT_DIMS, preferred_element_type=F32)
                        total = part if total is None else total + part
                target[a * tall : (a + 1) * tall, i * LANES : (i + 1) * LANES] = total.astype(target.dtype)
    s_all[...] = s_all[...] + jnp.dot(w_all[...], f_ref[...], preferred_element_type=F32)
    sums = [jnp.zeros((1, width), F32)] * 5
    for a in range(rows):
        x = x_ref[a].astype(F32)
        w = w_all[a * tall : (a + 1) * tall, :]
        w_ref[a] = w[:pairs]
        w = w.astype(F32)[:pairs]
        s = s_all[a * tall : a * tall + pairs, :]
        sigma_ref[a] = s
        for n, product in enumerate((x * s, x * w, s * s, s * w, w * w)):
            sums[n] = sums[n] + jnp.sum(product, axis=0, keepdims=True)
    lane = lax.broadcasted_iota(jnp.int32, (1, LANES), 1)
    packed = jnp.zeros((1, LANES), F32)
    for n in range(5):
        packed = packed + jnp.where(lane == n, jnp.sum(sums[n]), 0.0)
    sums_ref[...] = packed


def last(received, x, fock):
    rows, pairs, width = x.shape
    used = received.shape[1] // 2
    tall = (pairs + 7) // 8 * 8
    pitch = 2 * used + 8
    vmem = pl.BlockSpec(memory_space=pltpu.VMEM)
    return pl.pallas_call(
        functools.partial(last_kernel, pitch),
        out_shape=(
            jax.ShapeDtypeStruct((rows, pairs, width), F32),
            jax.ShapeDtypeStruct((rows, pairs, width), BF),
            jax.ShapeDtypeStruct((1, LANES), F32),
        ),
        in_specs=[vmem] * 3,
        out_specs=(vmem, vmem, vmem),
        scratch_shapes=[
            pltpu.VMEM((LANES * pitch, LANES), F32),
            pltpu.VMEM((rows * tall, width), BF),
            pltpu.VMEM((rows * tall, width), F32),
        ],
        compiler_params=pltpu.CompilerParams(vmem_limit_bytes=VMEM_LIMIT),
    )(received, x, fock)


def exchange(value):
    return lax.all_to_all(value, ALL, split_axis=0, concat_axis=0, tiled=True)


def local(amplitudes, virtual_fock_block, metric, active_block):
    acts = lax.axis_size("act")
    x = jnp.transpose(amplitudes, (1, 0, 2))
    rows, pairs, width = x.shape
    items = width // LANES
    arrived = exchange(pack(x))
    sent = middle(arrived, virtual_fock_block, metric, active_block, acts, rows, pairs, items)
    sigma, weighted, partial = last(exchange(sent), x, virtual_fock_block)
    spread = jnp.broadcast_to(partial[None], (LANES,) + partial.shape)
    totals = jnp.sum(exchange(spread), axis=(0, 1))
    denominator = totals[1]
    rayleigh = totals[0] / denominator
    resid = sigma - rayleigh * weighted.astype(F32)
    squares = totals[2] - 2.0 * rayleigh * totals[3] + rayleigh * rayleigh * totals[4]
    return jnp.transpose(resid.astype(BF), (1, 0, 2)), rayleigh, squares / denominator


def solution(mesh):
    in_specs = (P("act", "virt", None), P(), P(), P())
    out_specs = (P("act", "virt", None), P(), P())
    return jax.shard_map(local, mesh=mesh, in_specs=in_specs, out_specs=out_specs, check_vma=False)
```

profile of v0, /device:TPU:1, one launch (start us, length us, event | category | flops | bytes accessed | tf_op | source)
XLA Modules:
  0.0 187.4 jit_solution(18277817072398478767)
XLA Ops:
  0.6 5.1 %shard_map.67 = bf16[128,80,128]{2,1,0:T(8,128)(2,1)} custom-call(bf16[20,100,640]{2,1,0:T(8,128)(2,1)} %bitcast.10), custom_call_target="tpu_custom_call" | custom-call | tf_op jit(solution)/shard_map/pallas_call | solution.py:64
  5.8 47.2 %all_to_all.15.r_ref = bf16[128,80,128]{2,1,0:T(8,128)(2,1)} all-to-all(bf16[128,80,128]{2,1,0:T(8,128)(2,1)} %shard_map.67), channel_id=1, replica_groups=mesh['act'=4,'virt'=32] {'act','virt'}, dimensions={0} | all-to-all | bytes 5242880 | tf_op jit(solution)/shard_map/all_to_all | solution.py:224
  53.0 20.0 %shard_map.68 = bf16[128,160,128]{2,1,0:T(8,128)(2,1)} custom-call(bf16[128,80,128]{2,1,0:T(8,128)(2,1)} %all_to_all.15.r_ref, bf16[640,640]{1,0:T(8,128)(2,1)} %f_ref.3, bf16[400,400]{1,0:T(8,128)(2,1)} %m_ref.1, bf16[400,400]{1,0:T(8,128)(2,1)} %h_ref.1), custom_call_target="tpu_custom_call" | custom-call | tf_op jit(solution)/shard_map/pallas_call | solution.py:137
  73.0 70.0 %all_to_all.16.r_ref = bf16[128,160,128]{2,1,0:T(8,128)(2,1)} all-to-all(bf16[128,160,128]{2,1,0:T(8,128)(2,1)} %shard_map.68), channel_id=1, replica_groups=mesh['act'=4,'virt'=32] {'act','virt'}, dimensions={0} | all-to-all | bytes 10485760 | tf_op jit(solution)/shard_map/all_to_all | solution.py:224
  142.9 15.4 %shard_map.69 = (f32[20,100,640]{2,1,0:T(8,128)}, bf16[20,100,640]{2,1,0:T(8,128)(2,1)}, f32[1,128]{1,0:T(1,128)}) custom-call(bf16[128,160,128]{2,1,0:T(8,128)(2,1)} %all_to_all.16.r_ref, bf16[20,100,640]{2,1,0:T(8,128)(2,1)} %bitcast.11, bf16[640,640]{1,0:T(8,128)(2,1)} %f_ref.3), custom_call_target="tpu_custom_call" | custom-call | tf_op jit(solution)/shard_map/pallas_call | solution.py:205
  158.3 0.7 broadcast_in_dim.9
  159.0 15.9 %all_to_all.17 = f32[128,1,128]{2,1,0:T(1,128)S(1)} all-to-all(f32[128,1,128]{2,1,0:T(1,128)S(1)} %broadcast_in_dim.9), channel_id=1, replica_groups=mesh['act'=4,'virt'=32] {'act','virt'}, dimensions={0} | all-to-all | bytes 131072 | tf_op jit(solution)/shard_map/all_to_all | solution.py:224
  174.9 0.7 fusion.1
  179.6 5.6 %fusion = bf16[100,20,640]{2,0,1:T(8,128)(2,1)} fusion(f32[20,100,640]{2,1,0:T(8,128)} %get-tuple-element.6, bf16[20,100,640]{2,1,0:T(8,128)(2,1)} %get-tuple-element.8, f32[]{:T(128)} %div.6), kind=kLoop, calls=%fused_computation.1 | loop fusion | flops 5120000 | bytes 10240004 | tf_op jit(solution)/shard_map/transpose | solution.py:241
  (1 shorter events, 0.0 us)
where the time goes:
time: 188 us; the launch traced here: 187 us
  blocking collectives  133 us (71%)
  Pallas kernels  40.5 us (22%)
  between operations  6.84 us (4%)
  other arithmetic  5.62 us (3%)
    all_to_all x3, blocking collectives, exchange(): return lax.all_to_all(value, ALL, split_axis=0, concat_axis=0, tiled=True)  133 us
    pallas_call x1, Pallas kernels, middle(): pl.pallas_call(functools.partial(mid_kernel, acts, rows, pairs, items), o...  20 us
    pallas_call x1, Pallas kernels, last(): pl.pallas_call(functools.partial(last_kernel, pitch), out_shape=(jax.Shap...  15.4 us
    transpose x1, other arithmetic, local(): jnp.transpose(resid.astype(BF), (1, 0, 2))  5.59 us
    pallas_call x1, Pallas kernels, pack(): pl.pallas_call(functools.partial(pack_kernel, pitch), out_shape=jax.Shape...  5.13 us

commit v1 on v0

--- a/solution.py
+++ b/solution.py
@@ -12,7 +12,8 @@
 ALL = ("act", "virt")
 LANES = 128
 USED = 125
-VMEM_LIMIT = 60 * 1024 * 1024
+MIB = 1024 * 1024
+PACK_LIMIT, MID_LIMIT, LAST_LIMIT, FINISH_LIMIT = 16 * MIB, 40 * MIB, 44 * MIB, 16 * MIB
 NT_DIMS = (((1,), (1,)), ((), ()))
 TN_DIMS = (((0,), (0,)), ((), ()))
 
@@ -67,22 +68,45 @@
         in_specs=[pl.BlockSpec(memory_space=pltpu.VMEM)],
         out_specs=pl.BlockSpec(memory_space=pltpu.VMEM),
         scratch_shapes=[pltpu.VMEM((LANES * pitch, LANES), F32)],
-        compiler_params=pltpu.CompilerParams(vmem_limit_bytes=VMEM_LIMIT),
+        compiler_params=pltpu.CompilerParams(vmem_limit_bytes=PACK_LIMIT),
     )(x)
 
 
-def mid_kernel(
-    acts, rows, pairs, items, r_ref, f_ref, m_ref, h_ref, out_ref, flat, unsel, padded, u_ref, w_ref, s_ref
-):
+def pieces(item, pairs):
+    first, end = item * pairs, (item + 1) * pairs
+    return [
+        (k, max(first, k * USED) - first, min(end, (k + 1) * USED) - first)
+        for k in range(first // USED, (end - 1) // USED + 1)
+    ]
+
+
+def parts(chunk, pairs):
+    first, end = chunk * USED, (chunk + 1) * USED
+    return [
+        (i, max(first, i * pairs) - first, min(end, (i + 1) * pairs) - first)
+        for i in range(first // pairs, (end - 1) // pairs + 1)
+    ]
+
+
+def turned(tile, shift):
+    shift %= LANES
+    return tile if shift == 0 else pltpu.roll(tile, shift, 1)
+
+
+def joined(found, lane):
+    tile = found[0][0]
+    for other, first in found[1:]:
+        tile = jnp.where(lane >= first, other, tile)
+    return tile
+
+
+def mid_kernel(acts, rows, pairs, items, r_ref, f_ref, m_ref, h_ref, out_ref, flat, padded, u_ref, y_ref):
     count = r_ref.shape[0] // acts
     wide = count * rows
     chunks = pairs * items // USED
     used = chunks * rows
-    for k in range(chunks):
-        for i in range(items):
-            unsel[k * LANES : (k + 1) * LANES, i * LANES : (i + 1) * LANES] = onehot(
-                (LANES, LANES), k * USED, i * pairs, USED, pairs
-            )
+    span = acts * LANES
+    lane = lax.broadcasted_iota(jnp.int32, (wide, LANES), 1)
     for j in range(acts):
         padded[j * LANES : (j + 1) * LANES, :] = onehot((LANES, acts * pairs), j * pairs, 0, pairs, acts * pairs)
 
@@ -92,41 +116,36 @@
 
     m_wide = spread(m_ref[...])
     h_wide = spread(h_ref[...])
-
-    def arrive(j, carry):
+    for j in range(acts):
         for v in range(count):
             block = r_ref[j * count + v].astype(F32)
             for k in range(chunks):
                 flat[v * rows : (v + 1) * rows, k * LANES : (k + 1) * LANES] = block[k * rows : (k + 1) * rows]
-        u_ref[j] = jnp.dot(flat[...].astype(BF), unsel[...], preferred_element_type=F32).astype(BF)
-        return carry
-
-    lax.fori_loop(0, acts, arrive, 0)
+        for i in range(items):
+            found = [
+                (turned(flat[:, k * LANES : (k + 1) * LANES], k * USED - i * pairs), first)
+                for k, first, end in pieces(i, pairs)
+            ]
+            u_ref[i, :, j * LANES : (j + 1) * LANES] = joined(found, lane).astype(BF)
     for i in range(items):
-        cols = slice(i * LANES, (i + 1) * LANES)
-        u = jnp.concatenate([u_ref[j, :, cols] for j in range(acts)], axis=1)
-        w = jnp.dot(u, m_wide, preferred_element_type=F32).astype(BF)
-        s = jnp.dot(f_ref[...], w, preferred_element_type=F32)
-        s = (s + jnp.dot(u, h_wide, preferred_element_type=F32)).astype(BF)
-        for j in range(acts):
-            w_ref[j, :, cols] = w[:, j * LANES : (j + 1) * LANES]
-            s_ref[j, :, cols] = s[:, j * LANES : (j + 1) * LANES]
-
-    def leave(j, carry):
-        for n, source in enumerate((w_ref, s_ref)):
-            flat[...] = lax.dot_general(source[j], unsel[...], NT_DIMS, preferred_element_type=F32)
+        w = jnp.dot(u_ref[i], m_wide, preferred_element_type=F32)
+        y_ref[0, i] = w
+        s = jnp.dot(f_ref[...], w.astype(BF), preferred_element_type=F32)
+        y_ref[1, i] = s + jnp.dot(u_ref[i], h_wide, preferred_element_type=F32)
+    for j in range(acts):
+        for n in range(2):
+            for k in range(chunks):
+                found = [
+                    (turned(y_ref[n, i, :, j * LANES : (j + 1) * LANES], i * pairs - k * USED), first)
+                    for i, first, end in parts(k, pairs)
+                ]
+                flat[:, k * LANES : (k + 1) * LANES] = joined(found, lane)
             for v in range(count):
                 block = jnp.concatenate(
-                    [
-                        flat[v * rows : (v + 1) * rows, k * LANES : (k + 1) * LANES]
-                        for k in range(chunks)
-                    ],
+                    [flat[v * rows : (v + 1) * rows, k * LANES : (k + 1) * LANES] for k in range(chunks)],
                     axis=0,
                 )
                 out_ref[j * count + v, n * used : (n + 1) * used, :] = block.astype(BF)
-        return carry
-
-    lax.fori_loop(0, acts, leave, 0)
 
 
 def middle(received, fock, metric, active, acts, rows, pairs, items):
@@ -141,13 +160,11 @@
         out_specs=vmem,
         scratch_shapes=[
             pltpu.VMEM((wide, chunks * LANES), F32),
-            pltpu.VMEM((chunks * LANES, items * LANES), BF),
             pltpu.VMEM((acts * LANES, acts * pairs), BF),
-            pltpu.VMEM((acts, wide, items * LANES), BF),
-            pltpu.VMEM((acts, wide, items * LANES), BF),
-            pltpu.VMEM((acts, wide, items * LANES), BF),
+            pltpu.VMEM((items, wide, acts * LANES), BF),
+            pltpu.VMEM((2, items, wide, acts * LANES), F32),
         ],
-        compiler_params=pltpu.CompilerParams(vmem_limit_bytes=VMEM_LIMIT),
+        compiler_params=pltpu.CompilerParams(vmem_limit_bytes=MID_LIMIT),
     )(received, fock, metric, active)
 
 
@@ -156,28 +173,33 @@
     items = width // LANES
     chunks = pairs * items // USED
     used = chunks * rows
-    table = touching(pairs, items)
     tall = w_all.shape[0] // rows
     for d in range(LANES):
         scratch[d * pitch : d * pitch + 2 * used, :] = r_ref[d].astype(F32)
-    sel = {
-        (k, i): onehot((tall, LANES), i * pairs, k * USED, pairs, USED)
-        for k in range(chunks)
-        for i in table[k]
-    }
-    for a in range(rows):
+    sel = [
+        jnp.concatenate(
+            [onehot((tall, LANES), i * pairs, k * USED, pairs, USED) for k, first, end in pieces(i, pairs)],
+            axis=1,
+        )
+        for i in range(items)
+    ]
+    for a in range(0, rows, 2):
         for n, target in enumerate((w_all, s_all)):
             got = [
-                scratch[pl.ds(n * used + k * rows + a, LANES, stride=pitch), :].astype(BF)
+                jnp.concatenate(
+                    [scratch[pl.ds(n * used + k * rows + b, LANES, stride=pitch), :] for b in (a, a + 1)],
+                    axis=0,
+                ).astype(BF)
                 for k in range(chunks)
             ]
             for i in range(items):
-                total = None
-                for k in range(chunks):
-                    if i in table[k]:
-                        part = lax.dot_general(sel[k, i], got[k], NT_DIMS, preferred_element_type=F32)
-                        total = part if total is None else total + part
-                target[a * tall : (a + 1) * tall, i * LANES : (i + 1) * LANES] = total.astype(target.dtype)
+                source = jnp.concatenate([got[k] for k, first, end in pieces(i, pairs)], axis=1)
+                both = lax.dot_general(sel[i], source, NT_DIMS, preferred_element_type=F32)
+                both = both.astype(target.dtype)
+                for b in range(2):
+                    target[(a + b) * tall : (a + b + 1) * tall, i * LANES : (i + 1) * LANES] = both[
+                        :, b * LANES : (b + 1) * LANES
+                    ]
     s_all[...] = s_all[...] + jnp.dot(w_all[...], f_ref[...], preferred_element_type=F32)
     sums = [jnp.zeros((1, width), F32)] * 5
     for a in range(rows):
@@ -193,7 +215,8 @@
     packed = jnp.zeros((1, LANES), F32)
     for n in range(5):
         packed = packed + jnp.where(lane == n, jnp.sum(sums[n]), 0.0)
-    sums_ref[...] = packed
+    for d in range(sums_ref.shape[0]):
+        sums_ref[d] = packed
 
 
 def last(received, x, fock):
@@ -207,7 +230,7 @@
         out_shape=(
             jax.ShapeDtypeStruct((rows, pairs, width), F32),
             jax.ShapeDtypeStruct((rows, pairs, width), BF),
-            jax.ShapeDtypeStruct((1, LANES), F32),
+            jax.ShapeDtypeStruct((LANES, 1, LANES), F32),
         ),
         in_specs=[vmem] * 3,
         out_specs=(vmem, vmem, vmem),
@@ -216,8 +239,34 @@
             pltpu.VMEM((rows * tall, width), BF),
             pltpu.VMEM((rows * tall, width), F32),
         ],
-        compiler_params=pltpu.CompilerParams(vmem_limit_bytes=VMEM_LIMIT),
+        compiler_params=pltpu.CompilerParams(vmem_limit_bytes=LAST_LIMIT),
     )(received, x, fock)
+
+
+def finish_kernel(sums_ref, sigma_ref, w_ref, resid_ref, ratio_ref, norm_ref):
+    totals = jnp.sum(sums_ref[...], axis=0)
+    lane = lax.broadcasted_iota(jnp.int32, totals.shape, 1)
+    total = [jnp.sum(jnp.where(lane == n, totals, 0.0)) for n in range(5)]
+    rayleigh = jnp.full((1, LANES), total[0]) / jnp.full((1, LANES), total[1])
+    squares = total[2] - 2.0 * rayleigh * total[3] + rayleigh * rayleigh * total[4]
+    ratio_ref[...] = rayleigh
+    norm_ref[...] = squares / jnp.full((1, LANES), total[1])
+    width = sigma_ref.shape[2]
+    wide = jnp.concatenate([rayleigh] * (width // LANES), axis=1)
+    for a in range(sigma_ref.shape[0]):
+        resid_ref[a] = (sigma_ref[a] - wide * w_ref[a].astype(F32)).astype(BF)
+
+
+def finish(sums, sigma, weighted):
+    vmem = pl.BlockSpec(memory_space=pltpu.VMEM)
+    row = jax.ShapeDtypeStruct((1, LANES), F32)
+    return pl.pallas_call(
+        finish_kernel,
+        out_shape=(jax.ShapeDtypeStruct(weighted.shape, BF), row, row),
+        in_specs=[vmem] * 3,
+        out_specs=(vmem,) * 3,
+        compiler_params=pltpu.CompilerParams(vmem_limit_bytes=FINISH_LIMIT),
+    )(sums, sigma, weighted)
 
 
 def exchange(value):
@@ -232,13 +281,8 @@
     arrived = exchange(pack(x))
     sent = middle(arrived, virtual_fock_block, metric, active_block, acts, rows, pairs, items)
     sigma, weighted, partial = last(exchange(sent), x, virtual_fock_block)
-    spread = jnp.broadcast_to(partial[None], (LANES,) + partial.shape)
-    totals = jnp.sum(exchange(spread), axis=(0, 1))
-    denominator = totals[1]
-    rayleigh = totals[0] / denominator
-    resid = sigma - rayleigh * weighted.astype(F32)
-    squares = totals[2] - 2.0 * rayleigh * totals[3] + rayleigh * rayleigh * totals[4]
-    return jnp.transpose(resid.astype(BF), (1, 0, 2)), rayleigh, squares / denominator
+    resid, rayleigh, norm = finish(exchange(partial), sigma, weighted)
+    return jnp.transpose(resid, (1, 0, 2)), rayleigh[0, 0], norm[0, 0]
 
 
 def solution(mesh):

time: 188 us -> 163 us (0.87)
  Pallas kernels: 40.5 us -> 25.5 us
  between operations: 6.84 us -> 0.69 us
  other arithmetic: 5.62 us -> 0 us
  local copies, waits for them, and re-layouts: 1.36 us -> 4.28 us
    pallas_call x1, Pallas kernels: 20 us -> 9.35 us  [middle(): pl.pallas_call(functools.partial(mid_kernel, acts, rows, pairs, items), o...]
    transpose x1 -> x0, other arithmetic: 5.59 us -> none  [local(): jnp.transpose(resid.astype(BF), (1, 0, 2))]
    unnamed x0 -> x12, local copies, waits for them, and re-layouts: none -> 4.28 us
    pallas_call x1, Pallas kernels: 15.4 us -> 11.6 us  [last(): pl.pallas_call(functools.partial(last_kernel, pitch), out_shape=(jax.Shap...]
    pallas_call x1, Pallas kernels: 5.13 us -> 1.88 us  [pack(): pl.pallas_call(functools.partial(pack_kernel, pitch), out_shape=jax.Shape...]
    pallas_call x0 -> x1, Pallas kernels: none -> 2.7 us  [finish(): pl.pallas_call(finish_kernel, out_shape=(jax.ShapeDtypeStruct(weighted.sh...]
where the time goes in v1:
time: 163 us; the launch traced here: 162 us
  blocking collectives  132 us (81%)
  Pallas kernels  25.5 us (16%)
  local copies, waits for them, and re-layouts  4.28 us (3%)
    all_to_all x3, blocking collectives, exchange(): return lax.all_to_all(value, ALL, split_axis=0, concat_axis=0, tiled=True)  132 us
    pallas_call x1, Pallas kernels, last(): pl.pallas_call(functools.partial(last_kernel, pitch), out_shape=(jax.Shap...  11.6 us
    pallas_call x1, Pallas kernels, middle(): pl.pallas_call(functools.partial(mid_kernel, acts, rows, pairs, items), o...  9.35 us
    unnamed x12, local copies, waits for them, and re-layouts  4.28 us

profile of v1, /device:TPU:1, one launch (start us, length us, event | category | flops | bytes accessed | tf_op | source)
XLA Modules:
  0.0 162.5 jit_solution(1836257744157983356)
XLA Ops:
  0.6 0.0 copy-start
  0.6 1.7 %copy-done = bf16[100,20,640]{2,0,1:T(8,128)(2,1)S(1)} copy-done((bf16[100,20,640]{2,0,1:T(8,128)(2,1)S(1)}, bf16[100,20,640]{2,0,1:T(8,128)(2,1)}, u32[]{:S(2)}) %copy-start) | copy-done | bytes 2560024
  2.4 1.9 %shard_map.67 = bf16[128,80,128]{2,1,0:T(8,128)(2,1)S(1)} custom-call(bf16[20,100,640]{2,1,0:T(8,128)(2,1)S(1)} %bitcast.6), custom_call_target="tpu_custom_call" | custom-call | tf_op jit(solution)/shard_map/pallas_call | solution.py:65
  4.3 0.0 copy-start.3
  4.3 0.0 copy-start.4
  4.3 0.0 copy-start.5
  4.3 46.9 %all_to_all.15.r_ref = bf16[128,80,128]{2,1,0:T(8,128)(2,1)S(1)} all-to-all(bf16[128,80,128]{2,1,0:T(8,128)(2,1)S(1)} %shard_map.67), channel_id=1, replica_groups=mesh['act'=4,'virt'=32] {'act','virt'}, dimensions={0} | all-to-all | bytes 5242880 | tf_op jit(solution)/shard_map/all_to_all | solution.py:273
  51.3 0.0 copy-done.3
  51.3 0.0 copy-done.4
  51.3 0.0 copy-done.5
  51.3 9.3 %shard_map.68 = bf16[128,160,128]{2,1,0:T(8,128)(2,1)S(1)} custom-call(bf16[128,80,128]{2,1,0:T(8,128)(2,1)S(1)} %all_to_all.15.r_ref, bf16[640,640]{1,0:T(8,128)(2,1)S(1)} %copy-done.3, bf16[400,400]{1,0:T(8,128)(2,1)S(1)} %copy-done.4, bf16[400,400]{1,0:T(8,128)(2,1)S(1)} %copy-done.5), custom_call_target="tpu_custom_call" | custom-call | tf_op jit(solution)/shard_map/pallas_call | solution.py:156
  60.6 0.0 copy-start.1
  60.6 69.1 %all_to_all.16.r_ref = bf16[128,160,128]{2,1,0:T(8,128)(2,1)} all-to-all(bf16[128,160,128]{2,1,0:T(8,128)(2,1)S(1)} %shard_map.68), channel_id=1, replica_groups=mesh['act'=4,'virt'=32] {'act','virt'}, dimensions={0} | all-to-all | bytes 10485760 | tf_op jit(solution)/shard_map/all_to_all | solution.py:273
  129.8 0.0 copy-done.1
  129.8 11.6 %shard_map.69 = (f32[20,100,640]{2,1,0:T(8,128)}, bf16[20,100,640]{2,1,0:T(8,128)(2,1)S(1)}, f32[128,1,128]{2,1,0:T(1,128)S(1)}) custom-call(bf16[128,160,128]{2,1,0:T(8,128)(2,1)} %all_to_all.16.r_ref, bf16[20,100,640]{2,1,0:T(8,128)(2,1)S(1)} %bitcast.7, bf16[640,640]{1,0:T(8,128)(2,1)S(1)} %copy-done.3), custom_call_target="tpu_custom_call" | custom-call | tf_op jit(solution)/shard_map/pallas_call | solution.py:228
  141.4 15.9 %all_to_all.17.sums_ref = f32[128,1,128]{2,1,0:T(1,128)S(1)} all-to-all(f32[128,1,128]{2,1,0:T(1,128)S(1)} %get-tuple-element.9), channel_id=1, replica_groups=mesh['act'=4,'virt'=32] {'act','virt'}, dimensions={0} | all-to-all | bytes 131072 | tf_op jit(solution)/shard_map/all_to_all | solution.py:273
  157.2 0.0 copy-start.2
  157.2 2.5 %copy-done.2 = f32[20,100,640]{2,1,0:T(8,128)S(1)} copy-done((f32[20,100,640]{2,1,0:T(8,128)S(1)}, f32[20,100,640]{2,1,0:T(8,128)}, u32[]{:S(2)}) %copy-start.2) | copy-done | bytes 5120024
  159.8 2.7 %shard_map.70 = (bf16[20,100,640]{2,1,0:T(8,128)(2,1)}, f32[1,128]{1,0:T(1,128)}, f32[1,128]{1,0:T(1,128)}) custom-call(f32[128,1,128]{2,1,0:T(1,128)S(1)} %all_to_all.17.sums_ref, f32[20,100,640]{2,1,0:T(8,128)S(1)} %copy-done.2, bf16[20,100,640]{2,1,0:T(8,128)(2,1)S(1)} %get-tuple-element.11.w_ref), custom_call_target="tpu_custom_call" | custom-call | tf_op jit(solution)/shard_map/pallas_call | solution.py:263
Async XLA Ops:
  0.6 1.8 %copy-start = (bf16[100,20,640]{2,0,1:T(8,128)(2,1)S(1)}, bf16[100,20,640]{2,0,1:T(8,128)(2,1)}, u32[]{:S(2)}) copy-start(bf16[100,20,640]{2,0,1:T(8,128)(2,1)} %param.4) | copy-start | bytes 7680004
  4.3 47.0 %copy-start.3 = (bf16[640,640]{1,0:T(8,128)(2,1)S(1)}, bf16[640,640]{1,0:T(8,128)(2,1)}, u32[]{:S(2)}) copy-start(bf16[640,640]{1,0:T(8,128)(2,1)} %f_ref.3) | copy-start | bytes 2457604
  4.3 47.0 %copy-start.4 = (bf16[400,400]{1,0:T(8,128)(2,1)S(1)}, bf16[400,400]{1,0:T(8,128)(2,1)}, u32[]{:S(2)}) copy-start(bf16[400,400]{1,0:T(8,128)(2,1)} %m_ref.1) | copy-start | bytes 960004
  4.3 47.0 %copy-start.5 = (bf16[400,400]{1,0:T(8,128)(2,1)S(1)}, bf16[400,400]{1,0:T(8,128)(2,1)}, u32[]{:S(2)}) copy-start(bf16[400,400]{1,0:T(8,128)(2,1)} %h_ref.1) | copy-start | bytes 960004
  60.6 69.1 %copy-start.1 = (bf16[100,20,640]{2,0,1:T(8,128)(2,1)S(1)}, bf16[100,20,640]{2,0,1:T(8,128)(2,1)}, u32[]{:S(2)}) copy-start(bf16[100,20,640]{2,0,1:T(8,128)(2,1)} %param.4) | copy-start | bytes 7680004
  157.2 2.5 %copy-start.2 = (f32[20,100,640]{2,1,0:T(8,128)S(1)}, f32[20,100,640]{2,1,0:T(8,128)}, u32[]{:S(2)}) copy-start(f32[20,100,640]{2,1,0:T(8,128)} %get-tuple-element.10.sigma_ref) | copy-start | bytes 15360004

commit v2 on v1

v2 whole, which is shorter than its diff:
```python
import functools

import jax
import jax.numpy as jnp
from jax import lax
from jax.experimental import pallas as pl
from jax.experimental.pallas import tpu as pltpu
from jax.sharding import PartitionSpec as P

BF = jnp.bfloat16
F32 = jnp.float32
ALL = ("act", "virt")
LANES = 128
USED = 125
MIB = 1024 * 1024
PACK_LIMIT, MID_LIMIT, LAST_LIMIT, FINISH_LIMIT = 16 * MIB, 26 * MIB, 32 * MIB, 8 * MIB
LANES_ROWS = 104
NT_DIMS = (((1,), (1,)), ((), ()))
TN_DIMS = (((0,), (0,)), ((), ()))


def onehot(shape, row_base, column_base, row_end, column_end):
    rows = lax.broadcasted_iota(jnp.int32, shape, 0)
    columns = lax.broadcasted_iota(jnp.int32, shape, 1)
    same = (rows + row_base) == (columns + column_base)
    keep = same & (rows < row_end) & (columns < column_end)
    return jnp.where(keep, 1.0, 0.0).astype(BF)


def touching(pairs, items):
    chunks = pairs * items // USED
    return [
        [i for i in range(items) if i * pairs < (k + 1) * USED and (i + 1) * pairs > k * USED]
        for k in range(chunks)
    ]


def pack_kernel(acts, pitch, x_hbm, m_hbm, h_hbm, out_ref, wide_ref, x_ref, m_ref, h_ref, scratch, padded, sems):
    rows, pairs, width = x_hbm.shape
    items = width // LANES
    table = touching(pairs, items)
    chunks = len(table)
    pairs_of = ((m_hbm, m_ref), (h_hbm, h_ref), (x_hbm, x_ref))
    copies = [pltpu.make_async_copy(a, b, sems.at[n]) for n, (a, b) in enumerate(pairs_of)]
    for copy in copies:
        copy.start()
    span = acts * LANES
    for j in range(acts):
        padded[j * LANES : (j + 1) * LANES, :] = onehot((LANES, acts * pairs), j * pairs, 0, pairs, acts * pairs)
    for n, matrix in enumerate((m_ref, h_ref)):
        copies[n].wait()
        half = lax.dot_general(padded[...], matrix[...], NT_DIMS, preferred_element_type=F32).astype(BF)
        wide = lax.dot_general(half, padded[...], NT_DIMS, preferred_element_type=F32)
        wide_ref[:, n * span : (n + 1) * span] = wide.astype(BF)
    sel = {
        (k, i): onehot((pairs, LANES), i * pairs, k * USED, pairs, USED)
        for k in range(chunks)
        for i in table[k]
    }
    copies[2].wait()
    for a in range(rows):
        for k in range(chunks):
            total = None
            for i in table[k]:
                part = lax.dot_general(
                    x_ref[a, :, i * LANES : (i + 1) * LANES], sel[k, i], TN_DIMS, preferred_element_type=F32
                )
                total = part if total is None else total + part
            scratch[pl.ds(k * rows + a, LANES, stride=pitch), :] = total
    used = chunks * rows
    for d in range(LANES):
        out_ref[d] = scratch[d * pitch : d * pitch + used, :].astype(BF)


def pack(x, metric, active, acts):
    rows, pairs, width = x.shape
    used = pairs * (width // LANES) // USED * rows
    pitch = used + 8
    span = acts * LANES
    vmem = pl.BlockSpec(memory_space=pltpu.VMEM)
    return pl.pallas_call(
        functools.partial(pack_kernel, acts, pitch),
        out_shape=(
            jax.ShapeDtypeStruct((LANES, used, LANES), BF),
            jax.ShapeDtypeStruct((span, 2 * span), BF),
        ),
        in_specs=[pl.BlockSpec(memory_space=pltpu.HBM)] * 3,
        out_specs=(vmem, vmem),
        scratch_shapes=[
            pltpu.VMEM(x.shape, BF),
            pltpu.VMEM(metric.shape, BF),
            pltpu.VMEM(active.shape, BF),
            pltpu.VMEM((LANES * pitch, LANES), F32),
            pltpu.VMEM((span, acts * pairs), BF),
            pltpu.SemaphoreType.DMA((3,)),
        ],
        compiler_params=pltpu.CompilerParams(vmem_limit_bytes=PACK_LIMIT),
    )(*(pltpu.with_memory_space_constraint(a, pltpu.HBM) for a in (x, metric, active)))


def pieces(item, pairs):
    first, end = item * pairs, (item + 1) * pairs
    return [
        (k, max(first, k * USED) - first, min(end, (k + 1) * USED) - first)
        for k in range(first // USED, (end - 1) // USED + 1)
    ]


def parts(chunk, pairs):
    first, end = chunk * USED, (chunk + 1) * USED
    return [
        (i, max(first, i * pairs) - first, min(end, (i + 1) * pairs) - first)
        for i in range(first // pairs, (end - 1) // pairs + 1)
    ]


def turned(tile, shift):
    shift %= LANES
    return tile if shift == 0 else pltpu.roll(tile, shift, 1)


def joined(found, lane):
    tile = found[0][0]
    for other, first in found[1:]:
        tile = jnp.where(lane >= first, other, tile)
    return tile


def mid_kernel(acts, rows, pairs, items, r_ref, f_ref, wide_ref, out_ref, flat, u_ref, y_ref):
    count = r_ref.shape[0] // acts
    tall = count * rows
    chunks = pairs * items // USED
    used = chunks * rows
    lane = lax.broadcasted_iota(jnp.int32, (tall, LANES), 1)
    for j in range(acts):
        for v in range(count):
            block = r_ref[j * count + v].astype(F32)
            for k in range(chunks):
                flat[0, v * rows : (v + 1) * rows, k * LANES : (k + 1) * LANES] = block[k * rows : (k + 1) * rows]
        for i in range(items):
            found = [
                (turned(flat[0, :, k * LANES : (k + 1) * LANES], k * USED - i * pairs), first)
                for k, first, end in pieces(i, pairs)
            ]
            u_ref[i, :, j * LANES : (j + 1) * LANES] = joined(found, lane).astype(BF)
    for i in range(items):
        y_ref[i] = jnp.dot(u_ref[i], wide_ref[...], preferred_element_type=F32)
    for j in range(acts):
        for n in range(2):
            at = (n * acts + j) * LANES
            for k in range(chunks):
                found = [
                    (turned(y_ref[i, :, at : at + LANES], i * pairs - k * USED), first)
                    for i, first, end in parts(k, pairs)
                ]
                flat[n, :, k * LANES : (k + 1) * LANES] = joined(found, lane)
        flat[1] = flat[1] + jnp.dot(f_ref[...], flat[0].astype(BF), preferred_element_type=F32)
        for n in range(2):
            for v in range(count):
                block = jnp.concatenate(
                    [flat[n, v * rows : (v + 1) * rows, k * LANES : (k + 1) * LANES] for k in range(chunks)],
                    axis=0,
                )
                out_ref[j * count + v, n * used : (n + 1) * used, :] = block.astype(BF)


def middle(received, fock, wide, acts, rows, pairs, items):
    count = received.shape[0] // acts
    tall = count * rows
    chunks = pairs * items // USED
    vmem = pl.BlockSpec(memory_space=pltpu.VMEM)
    return pl.pallas_call(
        functools.partial(mid_kernel, acts, rows, pairs, items),
        out_shape=jax.ShapeDtypeStruct((LANES, 2 * chunks * rows, LANES), BF),
        in_specs=[vmem] * 3,
        out_specs=vmem,
        scratch_shapes=[
            pltpu.VMEM((2, tall, chunks * LANES), F32),
            pltpu.VMEM((items, tall, acts * LANES), BF),
            pltpu.VMEM((items, tall, 2 * acts * LANES), F32),
        ],
        compiler_params=pltpu.CompilerParams(vmem_limit_bytes=MID_LIMIT),
    )(received, fock, wide)


def last_kernel(pitch, r_ref, x_ref, f_ref, sigma_ref, w_ref, sums_ref, scratch, w_all, s_all):
    rows, pairs, width = x_ref.shape
    items = width // LANES
    chunks = pairs * items // USED
    used = chunks * rows
    group, tall = w_all.shape[0] // LANES_ROWS, LANES_ROWS
    whole = pairs // 8 * 8
    for d in range(LANES):
        scratch[d * pitch : d * pitch + 2 * used, :] = r_ref[d].astype(F32)
    sel = [
        jnp.concatenate(
            [onehot((tall, LANES), i * pairs, k * USED, pairs, USED) for k, first, end in pieces(i, pairs)],
            axis=1,
        )
        for i in range(items)
    ]
    sums = [jnp.zeros((8, width), F32)] * 5
    for base in range(0, rows, group):
        for a in range(0, group, 2):
            for n, target in enumerate((w_all, s_all)):
                got = [
                    jnp.concatenate(
                        [
                            scratch[pl.ds(n * used + k * rows + base + b, LANES, stride=pitch), :]
                            for b in (a, a + 1)
                        ],
                        axis=0,
                    ).astype(BF)
                    for k in range(chunks)
                ]
                for i in range(items):
                    source = jnp.concatenate([got[k] for k, first, end in pieces(i, pairs)], axis=1)
                    both = lax.dot_general(sel[i], source, NT_DIMS, preferred_element_type=F32)
                    both = both.astype(target.dtype)
                    for b in range(2):
                        target[(a + b) * tall : (a + b + 1) * tall, i * LANES : (i + 1) * LANES] = both[
                            :, b * LANES : (b + 1) * LANES
                        ]
        s_all[...] = s_all[...] + jnp.dot(w_all[...], f_ref[...], preferred_element_type=F32)
        for a in range(group):
            w_ref[base + a] = w_all[a * tall : a * tall + pairs, :]
            sigma_ref[base + a] = s_all[a * tall : a * tall + pairs, :]
            for first, end in ((0, whole), (whole, pairs)):
                x = x_ref[base + a, first:end].astype(F32)
                w = w_all[a * tall + first : a * tall + end, :].astype(F32)
                s = s_all[a * tall + first : a * tall + end, :]
                for n, product in enumerate((x * s, x * w, s * s, s * w, w * w)):
                    if end - first >= 8:
                        product = jnp.sum(product.reshape(-1, 8, width), axis=0)
                    else:
                        product = jnp.concatenate(
                            [product, jnp.zeros((8 - (end - first), width), F32)], axis=0
                        )
                    sums[n] = sums[n] + product
    lane = lax.broadcasted_iota(jnp.int32, (1, LANES), 1)
    packed = jnp.zeros((1, LANES), F32)
    for n in range(5):
        packed = packed + jnp.where(lane == n, jnp.sum(sums[n]), 0.0)
    for d in range(sums_ref.shape[0]):
        sums_ref[d] = packed


def last(received, x, fock):
    rows, pairs, width = x.shape
    used = received.shape[1] // 2
    pitch = 2 * used + 8
    group = rows
    vmem = pl.BlockSpec(memory_space=pltpu.VMEM)
    return pl.pallas_call(
        functools.partial(last_kernel, pitch),
        out_shape=(
            jax.ShapeDtypeStruct((rows, pairs, width), F32),
            jax.ShapeDtypeStruct((rows, pairs, width), BF),
            jax.ShapeDtypeStruct((LANES, 1, LANES), F32),
        ),
        in_specs=[vmem] * 3,
        out_specs=(vmem, vmem, vmem),
        scratch_shapes=[
            pltpu.VMEM((LANES * pitch, LANES), F32),
            pltpu.VMEM((group * LANES_ROWS, width), BF),
            pltpu.VMEM((group * LANES_ROWS, width), F32),
        ],
        compiler_params=pltpu.CompilerParams(vmem_limit_bytes=LAST_LIMIT),
    )(received, x, fock)


def finish_kernel(sums_ref, sigma_ref, w_ref, resid_hbm, ratio_ref, norm_ref, resid_ref, sems):
    totals = jnp.sum(sums_ref[...], axis=0)
    lane = lax.broadcasted_iota(jnp.int32, totals.shape, 1)
    total = [jnp.sum(jnp.where(lane == n, totals, 0.0)) for n in range(5)]
    rayleigh = jnp.full((1, LANES), total[0]) / jnp.full((1, LANES), total[1])
    squares = total[2] - 2.0 * rayleigh * total[3] + rayleigh * rayleigh * total[4]
    ratio_ref[...] = rayleigh
    norm_ref[...] = squares / jnp.full((1, LANES), total[1])
    rows, pairs, width = sigma_ref.shape
    wide = jnp.concatenate([rayleigh] * (width // LANES), axis=1)
    group = rows // sems.shape[0]
    copies = []
    for a in range(rows):
        resid_ref[a] = (sigma_ref[a] - wide * w_ref[a].astype(F32)).astype(BF)
        if (a + 1) % group == 0:
            part = pl.ds(a + 1 - group, group)
            copies.append(pltpu.make_async_copy(resid_ref.at[part], resid_hbm.at[part], sems.at[a // group]))
            copies[-1].start()
    for copy in copies:
        copy.wait()


def finish(sums, sigma, weighted):
    vmem = pl.BlockSpec(memory_space=pltpu.VMEM)
    row = jax.ShapeDtypeStruct((1, LANES), F32)
    return pl.pallas_call(
        finish_kernel,
        out_shape=(jax.ShapeDtypeStruct(weighted.shape, BF), row, row),
        in_specs=[vmem] * 3,
        out_specs=(pl.BlockSpec(memory_space=pltpu.HBM), vmem, vmem),
        scratch_shapes=[pltpu.VMEM(weighted.shape, BF), pltpu.SemaphoreType.DMA((5,))],
        compiler_params=pltpu.CompilerParams(vmem_limit_bytes=FINISH_LIMIT),
    )(sums, sigma, weighted)


def exchange(value):
    return lax.all_to_all(value, ALL, split_axis=0, concat_axis=0, tiled=True)


def local(amplitudes, virtual_fock_block, metric, active_block):
    acts = lax.axis_size("act")
    x = jnp.transpose(amplitudes, (1, 0, 2))
    rows, pairs, width = x.shape
    items = width // LANES
    packed, wide = pack(x, metric, active_block, acts)
    arrived = exchange(packed)
    sent = middle(arrived, virtual_fock_block, wide, acts, rows, pairs, items)
    sigma, weighted, partial = last(exchange(sent), x, virtual_fock_block)
    resid, rayleigh, norm = finish(exchange(partial), sigma, weighted)
    return jnp.transpose(resid, (1, 0, 2)), rayleigh[0, 0], norm[0, 0]


def solution(mesh):
    in_specs = (P("act", "virt", None), P(), P(), P())
    out_specs = (P("act", "virt", None), P(), P())
    return jax.shard_map(local, mesh=mesh, in_specs=in_specs, out_specs=out_specs, check_vma=False)
```

time: 163 us -> 155 us (0.951)
  local copies, waits for them, and re-layouts: 4.28 us -> 0.01 us
  Pallas kernels: 25.5 us -> 22.6 us
    unnamed x12 -> x4, local copies, waits for them, and re-layouts: 4.28 us -> 0.01 us
    pallas_call x1, Pallas kernels: 11.6 us -> 7.39 us  [last(): pl.pallas_call(functools.partial(last_kernel, pitch), out_shape=(jax.Shap...]
    pallas_call x1, Pallas kernels: 1.88 us -> 4.4 us  [pack(): pl.pallas_call(functools.partial(pack_kernel, acts, pitch), out_shape=(ja...]
where the time goes in v2:
time: 155 us
  blocking collectives  131 us (85%)
  Pallas kernels  22.6 us (15%)
    all_to_all x3, blocking collectives, exchange(): return lax.all_to_all(value, ALL, split_axis=0, concat_axis=0, tiled=True)  131 us
    pallas_call x1, Pallas kernels, middle(): pl.pallas_call(functools.partial(mid_kernel, acts, rows, pairs, items), o...  8.18 us
    pallas_call x1, Pallas kernels, last(): pl.pallas_call(functools.partial(last_kernel, pitch), out_shape=(jax.Shap...  7.39 us
    pallas_call x1, Pallas kernels, pack(): pl.pallas_call(functools.partial(pack_kernel, acts, pitch), out_shape=(ja...  4.4 us

profile of v2, /device:TPU:1, one launch (start us, length us, event | category | flops | bytes accessed | tf_op | source)
XLA Modules:
  0.0 154.6 jit_solution(121440958386735555)
XLA Ops:
  0.6 4.4 %shard_map.67 = (bf16[128,80,128]{2,1,0:T(8,128)(2,1)S(1)}, bf16[512,1024]{1,0:T(8,128)(2,1)S(1)}) custom-call(bf16[20,100,640]{2,1,0:T(8,128)(2,1)} %bitcast.6, bf16[400,400]{1,0:T(8,128)(2,1)} %m_hbm.1, bf16[400,400]{1,0:T(8,128)(2,1)} %h_hbm.1), custom_call_target="tpu_custom_call" | custom-call | tf_op jit(solution)/shard_map/pallas_call | solution.py:81
  5.0 0.0 copy-start.1
  5.0 46.9 %all_to_all.15.r_ref = bf16[128,80,128]{2,1,0:T(8,128)(2,1)S(1)} all-to-all(bf16[128,80,128]{2,1,0:T(8,128)(2,1)S(1)} %get-tuple-element.11), channel_id=1, replica_groups=mesh['act'=4,'virt'=32] {'act','virt'}, dimensions={0} | all-to-all | bytes 5242880 | tf_op jit(solution)/shard_map/all_to_all | solution.py:308
  52.0 0.0 copy-done.1
  52.0 8.2 %shard_map.68 = bf16[128,160,128]{2,1,0:T(8,128)(2,1)S(1)} custom-call(bf16[128,80,128]{2,1,0:T(8,128)(2,1)S(1)} %all_to_all.15.r_ref, bf16[640,640]{1,0:T(8,128)(2,1)S(1)} %copy-done.1, bf16[512,1024]{1,0:T(8,128)(2,1)S(1)} %get-tuple-element.12.wide_ref), custom_call_target="tpu_custom_call" | custom-call | tf_op jit(solution)/shard_map/pallas_call | solution.py:172
  60.2 0.0 copy-start
  60.2 68.4 %all_to_all.16.r_ref = bf16[128,160,128]{2,1,0:T(8,128)(2,1)S(1)} all-to-all(bf16[128,160,128]{2,1,0:T(8,128)(2,1)S(1)} %shard_map.68), channel_id=1, replica_groups=mesh['act'=4,'virt'=32] {'act','virt'}, dimensions={0} | all-to-all | bytes 10485760 | tf_op jit(solution)/shard_map/all_to_all | solution.py:308
  128.6 0.0 copy-done
  128.6 7.4 %shard_map.69 = (f32[20,100,640]{2,1,0:T(8,128)S(1)}, bf16[20,100,640]{2,1,0:T(8,128)(2,1)S(1)}, f32[128,1,128]{2,1,0:T(1,128)S(1)}) custom-call(bf16[128,160,128]{2,1,0:T(8,128)(2,1)S(1)} %all_to_all.16.r_ref, bf16[20,100,640]{2,1,0:T(8,128)(2,1)S(1)} %bitcast.7, bf16[640,640]{1,0:T(8,128)(2,1)S(1)} %copy-done.1), custom_call_target="tpu_custom_call" | custom-call | tf_op jit(solution)/shard_map/pallas_call | solution.py:254
  136.0 15.9 %all_to_all.17.sums_ref = f32[128,1,128]{2,1,0:T(1,128)S(1)} all-to-all(f32[128,1,128]{2,1,0:T(1,128)S(1)} %get-tuple-element.13), channel_id=1, replica_groups=mesh['act'=4,'virt'=32] {'act','virt'}, dimensions={0} | all-to-all | bytes 131072 | tf_op jit(solution)/shard_map/all_to_all | solution.py:308
  151.9 2.6 %shard_map.70 = (bf16[20,100,640]{2,1,0:T(8,128)(2,1)}, f32[1,128]{1,0:T(1,128)}, f32[1,128]{1,0:T(1,128)}) custom-call(f32[128,1,128]{2,1,0:T(1,128)S(1)} %all_to_all.17.sums_ref, f32[20,100,640]{2,1,0:T(8,128)S(1)} %get-tuple-element.14.sigma_ref, bf16[20,100,640]{2,1,0:T(8,128)(2,1)S(1)} %get-tuple-element.15.w_ref), custom_call_target="tpu_custom_call" | custom-call | tf_op jit(solution)/shard_map/pallas_call | solution.py:297
Async XLA Ops:
  5.0 47.0 %copy-start.1 = (bf16[640,640]{1,0:T(8,128)(2,1)S(1)}, bf16[640,640]{1,0:T(8,128)(2,1)}, u32[]{:S(2)}) copy-start(bf16[640,640]{1,0:T(8,128)(2,1)} %f_ref.3) | copy-start | bytes 2457604
  60.2 68.4 %copy-start = (bf16[100,20,640]{2,0,1:T(8,128)(2,1)S(1)}, bf16[100,20,640]{2,0,1:T(8,128)(2,1)}, u32[]{:S(2)}) copy-start(bf16[100,20,640]{2,0,1:T(8,128)(2,1)} %param.4) | copy-start | bytes 7680004

commit v3 on v2

--- a/solution.py
+++ b/solution.py
@@ -5,11 +5,13 @@
 from jax import lax
 from jax.experimental import pallas as pl
 from jax.experimental.pallas import tpu as pltpu
+from jax.sharding import Mesh
 from jax.sharding import PartitionSpec as P
 
 BF = jnp.bfloat16
 F32 = jnp.float32
-ALL = ("act", "virt")
+VIRT = ("virt_0", "virt_1", "core")
+ALL = ("core", "act", "virt_0", "virt_1")
 LANES = 128
 USED = 125
 MIB = 1024 * 1024
@@ -126,6 +128,10 @@
     return tile
 
 
+def place(j, v, acts, count):
+    return ((v % 2) * acts + j) * (count // 2) + v // 2
+
+
 def mid_kernel(acts, rows, pairs, items, r_ref, f_ref, wide_ref, out_ref, flat, u_ref, y_ref):
     count = r_ref.shape[0] // acts
     tall = count * rows
@@ -134,7 +140,7 @@
     lane = lax.broadcasted_iota(jnp.int32, (tall, LANES), 1)
     for j in range(acts):
         for v in range(count):
-            block = r_ref[j * count + v].astype(F32)
+            block = r_ref[place(j, v, acts, count)].astype(F32)
             for k in range(chunks):
                 flat[0, v * rows : (v + 1) * rows, k * LANES : (k + 1) * LANES] = block[k * rows : (k + 1) * rows]
         for i in range(items):
@@ -161,7 +167,7 @@
                     [flat[n, v * rows : (v + 1) * rows, k * LANES : (k + 1) * LANES] for k in range(chunks)],
                     axis=0,
                 )
-                out_ref[j * count + v, n * used : (n + 1) * used, :] = block.astype(BF)
+                out_ref[place(j, v, acts, count), n * used : (n + 1) * used, :] = block.astype(BF)
 
 
 def middle(received, fock, wide, acts, rows, pairs, items):
@@ -322,6 +328,8 @@
 
 
 def solution(mesh):
-    in_specs = (P("act", "virt", None), P(), P(), P())
-    out_specs = (P("act", "virt", None), P(), P())
-    return jax.shard_map(local, mesh=mesh, in_specs=in_specs, out_specs=out_specs, check_vma=False)
+    acts, virts = mesh.shape["act"], mesh.shape["virt"]
+    torus = Mesh(mesh.devices.reshape(acts, 4, virts // 8, 2), ("act",) + VIRT)
+    in_specs = (P("act", VIRT, None), P(), P(), P())
+    out_specs = (P("act", VIRT, None), P(), P())
+    return jax.shard_map(local, mesh=torus, in_specs=in_specs, out_specs=out_specs, check_vma=False)

time: 155 us -> 163 us (1.052)
  blocking collectives: 131 us -> 139 us
    all_to_all x3, blocking collectives: 131 us -> 139 us  [exchange(): return lax.all_to_all(value, ALL, split_axis=0, concat_axis=0, tiled=True)]
where the time goes in v3:
time: 163 us; the launch traced here: 162 us
  blocking collectives  139 us (85%)
  Pallas kernels  22.6 us (14%)
    all_to_all x3, blocking collectives, exchange(): return lax.all_to_all(value, ALL, split_axis=0, concat_axis=0, tiled=True)  139 us
    pallas_call x1, Pallas kernels, middle(): pl.pallas_call(functools.partial(mid_kernel, acts, rows, pairs, items), o...  8.21 us
    pallas_call x1, Pallas kernels, last(): pl.pallas_call(functools.partial(last_kernel, pitch), out_shape=(jax.Shap...  7.38 us
    pallas_call x1, Pallas kernels, pack(): pl.pallas_call(functools.partial(pack_kernel, acts, pitch), out_shape=(ja...  4.4 us

profile of v3, /device:TPU:1, one launch (start us, length us, event | category | flops | bytes accessed | tf_op | source)
XLA Modules:
  0.0 162.4 jit_solution(1666925294073836145)
XLA Ops:
  0.6 4.4 %shard_map.67 = (bf16[128,80,128]{2,1,0:T(8,128)(2,1)S(1)}, bf16[512,1024]{1,0:T(8,128)(2,1)S(1)}) custom-call(bf16[20,100,640]{2,1,0:T(8,128)(2,1)} %bitcast.6, bf16[400,400]{1,0:T(8,128)(2,1)} %m_hbm.1, bf16[400,400]{1,0:T(8,128)(2,1)} %h_hbm.1), custom_call_target="tpu_custom_call" | custom-call | tf_op jit(solution)/shard_map/pallas_call | solution.py:83
  5.0 0.0 copy-start.1
  5.0 45.5 %all_to_all.15.r_ref = bf16[128,80,128]{2,1,0:T(8,128)(2,1)S(1)} all-to-all(bf16[128,80,128]{2,1,0:T(8,128)(2,1)S(1)} %get-tuple-element.11), channel_id=1, replica_groups=mesh['act'=4,'virt_0'=4,'virt_1'=4,'core'=2] {'core','act','virt_0','vir..., dimensions={0} | all-to-all | bytes 5242880 | tf_op jit(solution)/shard_map/all_to_all | solution.py:314
  50.5 0.0 copy-done.1
  50.5 8.2 %shard_map.68 = bf16[128,160,128]{2,1,0:T(8,128)(2,1)S(1)} custom-call(bf16[128,80,128]{2,1,0:T(8,128)(2,1)S(1)} %all_to_all.15.r_ref, bf16[640,640]{1,0:T(8,128)(2,1)S(1)} %copy-done.1, bf16[512,1024]{1,0:T(8,128)(2,1)S(1)} %get-tuple-element.12.wide_ref), custom_call_target="tpu_custom_call" | custom-call | tf_op jit(solution)/shard_map/pallas_call | solution.py:178
  58.7 0.0 copy-start
  58.7 71.1 %all_to_all.16.r_ref = bf16[128,160,128]{2,1,0:T(8,128)(2,1)S(1)} all-to-all(bf16[128,160,128]{2,1,0:T(8,128)(2,1)S(1)} %shard_map.68), channel_id=1, replica_groups=mesh['act'=4,'virt_0'=4,'virt_1'=4,'core'=2] {'core','act','virt_0','vir..., dimensions={0} | all-to-all | bytes 10485760 | tf_op jit(solution)/shard_map/all_to_all | solution.py:314
  129.8 0.0 copy-done
  129.8 7.4 %shard_map.69 = (f32[20,100,640]{2,1,0:T(8,128)S(1)}, bf16[20,100,640]{2,1,0:T(8,128)(2,1)S(1)}, f32[128,1,128]{2,1,0:T(1,128)S(1)}) custom-call(bf16[128,160,128]{2,1,0:T(8,128)(2,1)S(1)} %all_to_all.16.r_ref, bf16[20,100,640]{2,1,0:T(8,128)(2,1)S(1)} %bitcast.7, bf16[640,640]{1,0:T(8,128)(2,1)S(1)} %copy-done.1), custom_call_target="tpu_custom_call" | custom-call | tf_op jit(solution)/shard_map/pallas_call | solution.py:260
  137.2 22.4 %all_to_all.17.sums_ref = f32[128,1,128]{2,1,0:T(1,128)S(1)} all-to-all(f32[128,1,128]{2,1,0:T(1,128)S(1)} %get-tuple-element.13), channel_id=1, replica_groups=mesh['act'=4,'virt_0'=4,'virt_1'=4,'core'=2] {'core','act','virt_0','vir..., dimensions={0} | all-to-all | bytes 131072 | tf_op jit(solution)/shard_map/all_to_all | solution.py:314
  159.6 2.6 %shard_map.70 = (bf16[20,100,640]{2,1,0:T(8,128)(2,1)}, f32[1,128]{1,0:T(1,128)}, f32[1,128]{1,0:T(1,128)}) custom-call(f32[128,1,128]{2,1,0:T(1,128)S(1)} %all_to_all.17.sums_ref, f32[20,100,640]{2,1,0:T(8,128)S(1)} %get-tuple-element.14.sigma_ref, bf16[20,100,640]{2,1,0:T(8,128)(2,1)S(1)} %get-tuple-element.15.w_ref), custom_call_target="tpu_custom_call" | custom-call | tf_op jit(solution)/shard_map/pallas_call | solution.py:303
Async XLA Ops:
  5.0 45.5 %copy-start.1 = (bf16[640,640]{1,0:T(8,128)(2,1)S(1)}, bf16[640,640]{1,0:T(8,128)(2,1)}, u32[]{:S(2)}) copy-start(bf16[640,640]{1,0:T(8,128)(2,1)} %f_ref.3) | copy-start | bytes 2457604
  58.7 71.1 %copy-start = (bf16[100,20,640]{2,0,1:T(8,128)(2,1)S(1)}, bf16[100,20,640]{2,0,1:T(8,128)(2,1)}, u32[]{:S(2)}) copy-start(bf16[100,20,640]{2,0,1:T(8,128)(2,1)} %param.4) | copy-start | bytes 7680004

commit v4 on v3

--- a/solution.py
+++ b/solution.py
@@ -11,7 +11,7 @@
 BF = jnp.bfloat16
 F32 = jnp.float32
 VIRT = ("virt_0", "virt_1", "core")
-ALL = ("core", "act", "virt_0", "virt_1")
+ALL = ("act", "core", "virt_0", "virt_1")
 LANES = 128
 USED = 125
 MIB = 1024 * 1024
@@ -128,8 +128,8 @@
     return tile
 
 
-def place(j, v, acts, count):
-    return ((v % 2) * acts + j) * (count // 2) + v // 2
+def place(j, v, count):
+    return (j * 2 + v % 2) * (count // 2) + v // 2
 
 
 def mid_kernel(acts, rows, pairs, items, r_ref, f_ref, wide_ref, out_ref, flat, u_ref, y_ref):
@@ -140,7 +140,7 @@
     lane = lax.broadcasted_iota(jnp.int32, (tall, LANES), 1)
     for j in range(acts):
         for v in range(count):
-            block = r_ref[place(j, v, acts, count)].astype(F32)
+            block = r_ref[place(j, v, count)].astype(F32)
             for k in range(chunks):
                 flat[0, v * rows : (v + 1) * rows, k * LANES : (k + 1) * LANES] = block[k * rows : (k + 1) * rows]
         for i in range(items):
@@ -167,7 +167,7 @@
                     [flat[n, v * rows : (v + 1) * rows, k * LANES : (k + 1) * LANES] for k in range(chunks)],
                     axis=0,
                 )
-                out_ref[place(j, v, acts, count), n * used : (n + 1) * used, :] = block.astype(BF)
+                out_ref[place(j, v, count), n * used : (n + 1) * used, :] = block.astype(BF)
 
 
 def middle(received, fock, wide, acts, rows, pairs, items):
@@ -189,7 +189,7 @@
     )(received, fock, wide)
 
 
-def last_kernel(pitch, r_ref, x_ref, f_ref, sigma_ref, w_ref, sums_ref, scratch, w_all, s_all):
+def last_kernel(pitch, r_ref, x_ref, f_ref, s_all, w_all, sums_ref, scratch):
     rows, pairs, width = x_ref.shape
     items = width // LANES
     chunks = pairs * items // USED
@@ -229,8 +229,6 @@
                         ]
         s_all[...] = s_all[...] + jnp.dot(w_all[...], f_ref[...], preferred_element_type=F32)
         for a in range(group):
-            w_ref[base + a] = w_all[a * tall : a * tall + pairs, :]
-            sigma_ref[base + a] = s_all[a * tall : a * tall + pairs, :]
             for first, end in ((0, whole), (whole, pairs)):
                 x = x_ref[base + a, first:end].astype(F32)
                 w = w_all[a * tall + first : a * tall + end, :].astype(F32)
@@ -255,21 +253,18 @@
     rows, pairs, width = x.shape
     used = received.shape[1] // 2
     pitch = 2 * used + 8
-    group = rows
     vmem = pl.BlockSpec(memory_space=pltpu.VMEM)
     return pl.pallas_call(
         functools.partial(last_kernel, pitch),
         out_shape=(
-            jax.ShapeDtypeStruct((rows, pairs, width), F32),
-            jax.ShapeDtypeStruct((rows, pairs, width), BF),
+            jax.ShapeDtypeStruct((rows * LANES_ROWS, width), F32),
+            jax.ShapeDtypeStruct((rows * LANES_ROWS, width), BF),
             jax.ShapeDtypeStruct((LANES, 1, LANES), F32),
         ),
         in_specs=[vmem] * 3,
         out_specs=(vmem, vmem, vmem),
         scratch_shapes=[
             pltpu.VMEM((LANES * pitch, LANES), F32),
-            pltpu.VMEM((group * LANES_ROWS, width), BF),
-            pltpu.VMEM((group * LANES_ROWS, width), F32),
         ],
         compiler_params=pltpu.CompilerParams(vmem_limit_bytes=LAST_LIMIT),
     )(received, x, fock)
@@ -283,12 +278,13 @@
     squares = total[2] - 2.0 * rayleigh * total[3] + rayleigh * rayleigh * total[4]
     ratio_ref[...] = rayleigh
     norm_ref[...] = squares / jnp.full((1, LANES), total[1])
-    rows, pairs, width = sigma_ref.shape
+    rows, pairs, width = resid_ref.shape
     wide = jnp.concatenate([rayleigh] * (width // LANES), axis=1)
     group = rows // sems.shape[0]
     copies = []
     for a in range(rows):
-        resid_ref[a] = (sigma_ref[a] - wide * w_ref[a].astype(F32)).astype(BF)
+        some = slice(a * LANES_ROWS, a * LANES_ROWS + pairs)
+        resid_ref[a] = (sigma_ref[some] - wide * w_ref[some].astype(F32)).astype(BF)
         if (a + 1) % group == 0:
             part = pl.ds(a + 1 - group, group)
             copies.append(pltpu.make_async_copy(resid_ref.at[part], resid_hbm.at[part], sems.at[a // group]))
@@ -297,15 +293,15 @@
         copy.wait()
 
 
-def finish(sums, sigma, weighted):
+def finish(sums, sigma, weighted, shape):
     vmem = pl.BlockSpec(memory_space=pltpu.VMEM)
     row = jax.ShapeDtypeStruct((1, LANES), F32)
     return pl.pallas_call(
         finish_kernel,
-        out_shape=(jax.ShapeDtypeStruct(weighted.shape, BF), row, row),
+        out_shape=(jax.ShapeDtypeStruct(shape, BF), row, row),
         in_specs=[vmem] * 3,
         out_specs=(pl.BlockSpec(memory_space=pltpu.HBM), vmem, vmem),
-        scratch_shapes=[pltpu.VMEM(weighted.shape, BF), pltpu.SemaphoreType.DMA((5,))],
+        scratch_shapes=[pltpu.VMEM(shape, BF), pltpu.SemaphoreType.DMA((5,))],
         compiler_params=pltpu.CompilerParams(vmem_limit_bytes=FINISH_LIMIT),
     )(sums, sigma, weighted)
 
@@ -323,7 +319,7 @@
     arrived = exchange(packed)
     sent = middle(arrived, virtual_fock_block, wide, acts, rows, pairs, items)
     sigma, weighted, partial = last(exchange(sent), x, virtual_fock_block)
-    resid, rayleigh, norm = finish(exchange(partial), sigma, weighted)
+    resid, rayleigh, norm = finish(exchange(partial), sigma, weighted, x.shape)
     return jnp.transpose(resid, (1, 0, 2)), rayleigh[0, 0], norm[0, 0]
 
 

time: 163 us -> 152 us (0.933)
  blocking collectives: 139 us -> 128 us
    all_to_all x3, blocking collectives: 139 us -> 128 us  [exchange(): return lax.all_to_all(value, ALL, split_axis=0, concat_axis=0, tiled=True)]
where the time goes in v4:
time: 152 us
  blocking collectives  128 us (84%)
  Pallas kernels  22.7 us (15%)
    all_to_all x3, blocking collectives, exchange(): return lax.all_to_all(value, ALL, split_axis=0, concat_axis=0, tiled=True)  128 us
    pallas_call x1, Pallas kernels, middle(): pl.pallas_call(functools.partial(mid_kernel, acts, rows, pairs, items), o...  8.21 us
    pallas_call x1, Pallas kernels, last(): pl.pallas_call(functools.partial(last_kernel, pitch), out_shape=(jax.Shap...  7.52 us
    pallas_call x1, Pallas kernels, pack(): pl.pallas_call(functools.partial(pack_kernel, acts, pitch), out_shape=(ja...  4.4 us

profile of v4, /device:TPU:1, one launch (start us, length us, event | category | flops | bytes accessed | tf_op | source)
XLA Modules:
  0.0 152.0 jit_solution(12805232264487546410)
XLA Ops:
  0.6 4.4 %shard_map.67 = (bf16[128,80,128]{2,1,0:T(8,128)(2,1)S(1)}, bf16[512,1024]{1,0:T(8,128)(2,1)S(1)}) custom-call(bf16[20,100,640]{2,1,0:T(8,128)(2,1)} %bitcast.6, bf16[400,400]{1,0:T(8,128)(2,1)} %m_hbm.1, bf16[400,400]{1,0:T(8,128)(2,1)} %h_hbm.1), custom_call_target="tpu_custom_call" | custom-call | tf_op jit(solution)/shard_map/pallas_call | solution.py:83
  5.0 0.0 copy-start.1
  5.0 46.5 %all_to_all.15.r_ref = bf16[128,80,128]{2,1,0:T(8,128)(2,1)S(1)} all-to-all(bf16[128,80,128]{2,1,0:T(8,128)(2,1)S(1)} %get-tuple-element.11), channel_id=1, replica_groups=mesh['act'=4,'virt_0'=4,'virt_1'=4,'core'=2] {'act','core','virt_0','vir..., dimensions={0} | all-to-all | bytes 5242880 | tf_op jit(solution)/shard_map/all_to_all | solution.py:310
  51.5 0.0 copy-done.1
  51.5 8.2 %shard_map.68 = bf16[128,160,128]{2,1,0:T(8,128)(2,1)S(1)} custom-call(bf16[128,80,128]{2,1,0:T(8,128)(2,1)S(1)} %all_to_all.15.r_ref, bf16[640,640]{1,0:T(8,128)(2,1)S(1)} %copy-done.1, bf16[512,1024]{1,0:T(8,128)(2,1)S(1)} %get-tuple-element.12.wide_ref), custom_call_target="tpu_custom_call" | custom-call | tf_op jit(solution)/shard_map/pallas_call | solution.py:178
  59.7 0.0 copy-start
  59.7 68.1 %all_to_all.16.r_ref = bf16[128,160,128]{2,1,0:T(8,128)(2,1)S(1)} all-to-all(bf16[128,160,128]{2,1,0:T(8,128)(2,1)S(1)} %shard_map.68), channel_id=1, replica_groups=mesh['act'=4,'virt_0'=4,'virt_1'=4,'core'=2] {'act','core','virt_0','vir..., dimensions={0} | all-to-all | bytes 10485760 | tf_op jit(solution)/shard_map/all_to_all | solution.py:310
  127.8 0.0 copy-done
  127.8 7.5 %shard_map.69 = (f32[2080,640]{1,0:T(8,128)S(1)}, bf16[2080,640]{1,0:T(8,128)(2,1)S(1)}, f32[128,1,128]{2,1,0:T(1,128)S(1)}) custom-call(bf16[128,160,128]{2,1,0:T(8,128)(2,1)S(1)} %all_to_all.16.r_ref, bf16[20,100,640]{2,1,0:T(8,128)(2,1)S(1)} %bitcast.7, bf16[640,640]{1,0:T(8,128)(2,1)S(1)} %copy-done.1), custom_call_target="tpu_custom_call" | custom-call | tf_op jit(solution)/shard_map/pallas_call | solution.py:257
  135.4 13.9 %all_to_all.17.sums_ref = f32[128,1,128]{2,1,0:T(1,128)S(1)} all-to-all(f32[128,1,128]{2,1,0:T(1,128)S(1)} %get-tuple-element.13), channel_id=1, replica_groups=mesh['act'=4,'virt_0'=4,'virt_1'=4,'core'=2] {'act','core','virt_0','vir..., dimensions={0} | all-to-all | bytes 131072 | tf_op jit(solution)/shard_map/all_to_all | solution.py:310
  149.3 2.6 %shard_map.70 = (bf16[20,100,640]{2,1,0:T(8,128)(2,1)}, f32[1,128]{1,0:T(1,128)}, f32[1,128]{1,0:T(1,128)}) custom-call(f32[128,1,128]{2,1,0:T(1,128)S(1)} %all_to_all.17.sums_ref, f32[2080,640]{1,0:T(8,128)S(1)} %get-tuple-element.14.sigma_ref, bf16[2080,640]{1,0:T(8,128)(2,1)S(1)} %get-tuple-element.15.w_ref), custom_call_target="tpu_custom_call" | custom-call | tf_op jit(solution)/shard_map/pallas_call | solution.py:299
Async XLA Ops:
  5.0 46.5 %copy-start.1 = (bf16[640,640]{1,0:T(8,128)(2,1)S(1)}, bf16[640,640]{1,0:T(8,128)(2,1)}, u32[]{:S(2)}) copy-start(bf16[640,640]{1,0:T(8,128)(2,1)} %f_ref.3) | copy-start | bytes 2457604
  59.7 68.1 %copy-start = (bf16[100,20,640]{2,0,1:T(8,128)(2,1)S(1)}, bf16[100,20,640]{2,0,1:T(8,128)(2,1)}, u32[]{:S(2)}) copy-start(bf16[100,20,640]{2,0,1:T(8,128)(2,1)} %param.4) | copy-start | bytes 7680004

commit v5 on v4

--- a/solution.py
+++ b/solution.py
@@ -92,7 +92,7 @@
             pltpu.VMEM(x.shape, BF),
             pltpu.VMEM(metric.shape, BF),
             pltpu.VMEM(active.shape, BF),
-            pltpu.VMEM((LANES * pitch, LANES), F32),
+            pltpu.VMEM(((LANES + 1) * pitch, LANES), F32),
             pltpu.VMEM((span, acts * pairs), BF),
             pltpu.SemaphoreType.DMA((3,)),
         ],
@@ -145,7 +145,7 @@
                 flat[0, v * rows : (v + 1) * rows, k * LANES : (k + 1) * LANES] = block[k * rows : (k + 1) * rows]
         for i in range(items):
             found = [
-                (turned(flat[0, :, k * LANES : (k + 1) * LANES], k * USED - i * pairs), first)
+                (turned(flat[0, :tall, k * LANES : (k + 1) * LANES], k * USED - i * pairs), first)
                 for k, first, end in pieces(i, pairs)
             ]
             u_ref[i, :, j * LANES : (j + 1) * LANES] = joined(found, lane).astype(BF)
@@ -159,8 +159,9 @@
                     (turned(y_ref[i, :, at : at + LANES], i * pairs - k * USED), first)
                     for i, first, end in parts(k, pairs)
                 ]
-                flat[n, :, k * LANES : (k + 1) * LANES] = joined(found, lane)
-        flat[1] = flat[1] + jnp.dot(f_ref[...], flat[0].astype(BF), preferred_element_type=F32)
+                flat[n, :tall, k * LANES : (k + 1) * LANES] = joined(found, lane)
+        right = jnp.dot(f_ref[...], flat[0, :tall].astype(BF), preferred_element_type=F32)
+        flat[1, :tall] = flat[1, :tall] + right
         for n in range(2):
             for v in range(count):
                 block = jnp.concatenate(
@@ -181,7 +182,7 @@
         in_specs=[vmem] * 3,
         out_specs=vmem,
         scratch_shapes=[
-            pltpu.VMEM((2, tall, chunks * LANES), F32),
+            pltpu.VMEM((2, tall + 8, chunks * LANES), F32),
             pltpu.VMEM((items, tall, acts * LANES), BF),
             pltpu.VMEM((items, tall, 2 * acts * LANES), F32),
         ],
@@ -198,12 +199,23 @@
     whole = pairs // 8 * 8
     for d in range(LANES):
         scratch[d * pitch : d * pitch + 2 * used, :] = r_ref[d].astype(F32)
+    covers = [((k, k + 1), []) for k in range(0, chunks, 2)]
+    for i in range(items):
+        need = tuple(k for k, first, end in pieces(i, pairs))
+        fits = [served for held, served in covers if set(need) <= set(held)]
+        if fits:
+            fits[0].append(i)
+        else:
+            covers.append((need, [i]))
     sel = [
         jnp.concatenate(
-            [onehot((tall, LANES), i * pairs, k * USED, pairs, USED) for k, first, end in pieces(i, pairs)],
-            axis=1,
+            [
+                jnp.concatenate([onehot((tall, LANES), i * pairs, k * USED, pairs, USED) for k in held], axis=1)
+                for i in served
+            ],
+            axis=0,
         )
-        for i in range(items)
+        for held, served in covers
     ]
     sums = [jnp.zeros((8, width), F32)] * 5
     for base in range(0, rows, group):
@@ -219,14 +231,15 @@
                     ).astype(BF)
                     for k in range(chunks)
                 ]
-                for i in range(items):
-                    source = jnp.concatenate([got[k] for k, first, end in pieces(i, pairs)], axis=1)
-                    both = lax.dot_general(sel[i], source, NT_DIMS, preferred_element_type=F32)
+                for rows_of, (held, served) in zip(sel, covers):
+                    source = jnp.concatenate([got[k] for k in held], axis=1)
+                    both = lax.dot_general(rows_of, source, NT_DIMS, preferred_element_type=F32)
                     both = both.astype(target.dtype)
-                    for b in range(2):
-                        target[(a + b) * tall : (a + b + 1) * tall, i * LANES : (i + 1) * LANES] = both[
-                            :, b * LANES : (b + 1) * LANES
-                        ]
+                    for n_item, i in enumerate(served):
+                        for b in range(2):
+                            target[(a + b) * tall : (a + b + 1) * tall, i * LANES : (i + 1) * LANES] = both[
+                                n_item * tall : (n_item + 1) * tall, b * LANES : (b + 1) * LANES
+                            ]
         s_all[...] = s_all[...] + jnp.dot(w_all[...], f_ref[...], preferred_element_type=F32)
         for a in range(group):
             for first, end in ((0, whole), (whole, pairs)):
@@ -264,7 +277,7 @@
         in_specs=[vmem] * 3,
         out_specs=(vmem, vmem, vmem),
         scratch_shapes=[
-            pltpu.VMEM((LANES * pitch, LANES), F32),
+            pltpu.VMEM(((LANES + 1) * pitch, LANES), F32),
         ],
         compiler_params=pltpu.CompilerParams(vmem_limit_bytes=LAST_LIMIT),
     )(received, x, fock)
@@ -301,7 +314,7 @@
         out_shape=(jax.ShapeDtypeStruct(shape, BF), row, row),
         in_specs=[vmem] * 3,
         out_specs=(pl.BlockSpec(memory_space=pltpu.HBM), vmem, vmem),
-        scratch_shapes=[pltpu.VMEM(shape, BF), pltpu.SemaphoreType.DMA((5,))],
+        scratch_shapes=[pltpu.VMEM(shape, BF), pltpu.SemaphoreType.DMA((10,))],
         compiler_params=pltpu.CompilerParams(vmem_limit_bytes=FINISH_LIMIT),
     )(sums, sigma, weighted)
 

time: 152 us -> 152 us (level)
  no operation moved by 1% of the time
where the time goes in v5:
time: 152 us
  blocking collectives  128 us (84%)
  Pallas kernels  22.7 us (15%)
    all_to_all x3, blocking collectives, exchange(): return lax.all_to_all(value, ALL, split_axis=0, concat_axis=0, tiled=True)  128 us
    pallas_call x1, Pallas kernels, middle(): pl.pallas_call(functools.partial(mid_kernel, acts, rows, pairs, items), o...  8.21 us
    pallas_call x1, Pallas kernels, last(): pl.pallas_call(functools.partial(last_kernel, pitch), out_shape=(jax.Shap...  7.51 us
    pallas_call x1, Pallas kernels, pack(): pl.pallas_call(functools.partial(pack_kernel, acts, pitch), out_shape=(ja...  4.4 us

profile of v5, /device:TPU:1, one launch (start us, length us, event | category | flops | bytes accessed | tf_op | source)
XLA Modules:
  0.0 152.0 jit_solution(17439060128758564675)
XLA Ops:
  0.6 4.4 %shard_map.67 = (bf16[128,80,128]{2,1,0:T(8,128)(2,1)S(1)}, bf16[512,1024]{1,0:T(8,128)(2,1)S(1)}) custom-call(bf16[20,100,640]{2,1,0:T(8,128)(2,1)} %bitcast.6, bf16[400,400]{1,0:T(8,128)(2,1)} %m_hbm.1, bf16[400,400]{1,0:T(8,128)(2,1)} %h_hbm.1), custom_call_target="tpu_custom_call" | custom-call | tf_op jit(solution)/shard_map/pallas_call | solution.py:83
  5.0 0.0 copy-start.1
  5.1 46.5 %all_to_all.15.r_ref = bf16[128,80,128]{2,1,0:T(8,128)(2,1)S(1)} all-to-all(bf16[128,80,128]{2,1,0:T(8,128)(2,1)S(1)} %get-tuple-element.11), channel_id=1, replica_groups=mesh['act'=4,'virt_0'=4,'virt_1'=4,'core'=2] {'act','core','virt_0','vir..., dimensions={0} | all-to-all | bytes 5242880 | tf_op jit(solution)/shard_map/all_to_all | solution.py:323
  51.5 0.0 copy-done.1
  51.5 8.2 %shard_map.68 = bf16[128,160,128]{2,1,0:T(8,128)(2,1)S(1)} custom-call(bf16[128,80,128]{2,1,0:T(8,128)(2,1)S(1)} %all_to_all.15.r_ref, bf16[640,640]{1,0:T(8,128)(2,1)S(1)} %copy-done.1, bf16[512,1024]{1,0:T(8,128)(2,1)S(1)} %get-tuple-element.12.wide_ref), custom_call_target="tpu_custom_call" | custom-call | tf_op jit(solution)/shard_map/pallas_call | solution.py:179
  59.7 0.0 copy-start
  59.7 68.1 %all_to_all.16.r_ref = bf16[128,160,128]{2,1,0:T(8,128)(2,1)S(1)} all-to-all(bf16[128,160,128]{2,1,0:T(8,128)(2,1)S(1)} %shard_map.68), channel_id=1, replica_groups=mesh['act'=4,'virt_0'=4,'virt_1'=4,'core'=2] {'act','core','virt_0','vir..., dimensions={0} | all-to-all | bytes 10485760 | tf_op jit(solution)/shard_map/all_to_all | solution.py:323
  127.9 0.0 copy-done
  127.9 7.5 %shard_map.69 = (f32[2080,640]{1,0:T(8,128)S(1)}, bf16[2080,640]{1,0:T(8,128)(2,1)S(1)}, f32[128,1,128]{2,1,0:T(1,128)S(1)}) custom-call(bf16[128,160,128]{2,1,0:T(8,128)(2,1)S(1)} %all_to_all.16.r_ref, bf16[20,100,640]{2,1,0:T(8,128)(2,1)S(1)} %bitcast.7, bf16[640,640]{1,0:T(8,128)(2,1)S(1)} %copy-done.1), custom_call_target="tpu_custom_call" | custom-call | tf_op jit(solution)/shard_map/pallas_call | solution.py:270
  135.4 13.9 %all_to_all.17.sums_ref = f32[128,1,128]{2,1,0:T(1,128)S(1)} all-to-all(f32[128,1,128]{2,1,0:T(1,128)S(1)} %get-tuple-element.13), channel_id=1, replica_groups=mesh['act'=4,'virt_0'=4,'virt_1'=4,'core'=2] {'act','core','virt_0','vir..., dimensions={0} | all-to-all | bytes 131072 | tf_op jit(solution)/shard_map/all_to_all | solution.py:323
  149.3 2.5 %shard_map.70 = (bf16[20,100,640]{2,1,0:T(8,128)(2,1)}, f32[1,128]{1,0:T(1,128)}, f32[1,128]{1,0:T(1,128)}) custom-call(f32[128,1,128]{2,1,0:T(1,128)S(1)} %all_to_all.17.sums_ref, f32[2080,640]{1,0:T(8,128)S(1)} %get-tuple-element.14.sigma_ref, bf16[2080,640]{1,0:T(8,128)(2,1)S(1)} %get-tuple-element.15.w_ref), custom_call_target="tpu_custom_call" | custom-call | tf_op jit(solution)/shard_map/pallas_call | solution.py:312
Async XLA Ops:
  5.0 46.5 %copy-start.1 = (bf16[640,640]{1,0:T(8,128)(2,1)S(1)}, bf16[640,640]{1,0:T(8,128)(2,1)}, u32[]{:S(2)}) copy-start(bf16[640,640]{1,0:T(8,128)(2,1)} %f_ref.3) | copy-start | bytes 2457604
  59.7 68.1 %copy-start = (bf16[100,20,640]{2,0,1:T(8,128)(2,1)S(1)}, bf16[100,20,640]{2,0,1:T(8,128)(2,1)}, u32[]{:S(2)}) copy-start(bf16[100,20,640]{2,0,1:T(8,128)(2,1)} %param.4) | copy-start | bytes 7680004

commit v6 on v5

--- a/solution.py
+++ b/solution.py
@@ -265,7 +265,7 @@
 def last(received, x, fock):
     rows, pairs, width = x.shape
     used = received.shape[1] // 2
-    pitch = 2 * used + 8
+    pitch = 2 * used + 4
     vmem = pl.BlockSpec(memory_space=pltpu.VMEM)
     return pl.pallas_call(
         functools.partial(last_kernel, pitch),

time: 152 us -> 152 us (level)
  no operation moved by 1% of the time
where the time goes in v6:
time: 152 us
  blocking collectives  128 us (84%)
  Pallas kernels  22.2 us (15%)
    all_to_all x3, blocking collectives, exchange(): return lax.all_to_all(value, ALL, split_axis=0, concat_axis=0, tiled=True)  128 us
    pallas_call x1, Pallas kernels, middle(): pl.pallas_call(functools.partial(mid_kernel, acts, rows, pairs, items), o...  8.21 us
    pallas_call x1, Pallas kernels, last(): pl.pallas_call(functools.partial(last_kernel, pitch), out_shape=(jax.Shap...  7.04 us
    pallas_call x1, Pallas kernels, pack(): pl.pallas_call(functools.partial(pack_kernel, acts, pitch), out_shape=(ja...  4.4 us

profile of v6, /device:TPU:1, one launch (start us, length us, event | category | flops | bytes accessed | tf_op | source)
XLA Modules:
  0.0 151.5 jit_solution(17153222582903370386)
XLA Ops:
  0.6 4.4 %shard_map.67 = (bf16[128,80,128]{2,1,0:T(8,128)(2,1)S(1)}, bf16[512,1024]{1,0:T(8,128)(2,1)S(1)}) custom-call(bf16[20,100,640]{2,1,0:T(8,128)(2,1)} %bitcast.6, bf16[400,400]{1,0:T(8,128)(2,1)} %m_hbm.1, bf16[400,400]{1,0:T(8,128)(2,1)} %h_hbm.1), custom_call_target="tpu_custom_call" | custom-call | tf_op jit(solution)/shard_map/pallas_call | solution.py:83
  5.0 0.0 copy-start.1
  5.1 46.5 %all_to_all.15.r_ref = bf16[128,80,128]{2,1,0:T(8,128)(2,1)S(1)} all-to-all(bf16[128,80,128]{2,1,0:T(8,128)(2,1)S(1)} %get-tuple-element.11), channel_id=1, replica_groups=mesh['act'=4,'virt_0'=4,'virt_1'=4,'core'=2] {'act','core','virt_0','vir..., dimensions={0} | all-to-all | bytes 5242880 | tf_op jit(solution)/shard_map/all_to_all | solution.py:323
  51.5 0.0 copy-done.1
  51.5 8.2 %shard_map.68 = bf16[128,160,128]{2,1,0:T(8,128)(2,1)S(1)} custom-call(bf16[128,80,128]{2,1,0:T(8,128)(2,1)S(1)} %all_to_all.15.r_ref, bf16[640,640]{1,0:T(8,128)(2,1)S(1)} %copy-done.1, bf16[512,1024]{1,0:T(8,128)(2,1)S(1)} %get-tuple-element.12.wide_ref), custom_call_target="tpu_custom_call" | custom-call | tf_op jit(solution)/shard_map/pallas_call | solution.py:179
  59.7 0.0 copy-start
  59.7 68.1 %all_to_all.16.r_ref = bf16[128,160,128]{2,1,0:T(8,128)(2,1)S(1)} all-to-all(bf16[128,160,128]{2,1,0:T(8,128)(2,1)S(1)} %shard_map.68), channel_id=1, replica_groups=mesh['act'=4,'virt_0'=4,'virt_1'=4,'core'=2] {'act','core','virt_0','vir..., dimensions={0} | all-to-all | bytes 10485760 | tf_op jit(solution)/shard_map/all_to_all | solution.py:323
  127.9 0.0 copy-done
  127.9 7.0 %shard_map.69 = (f32[2080,640]{1,0:T(8,128)S(1)}, bf16[2080,640]{1,0:T(8,128)(2,1)S(1)}, f32[128,1,128]{2,1,0:T(1,128)S(1)}) custom-call(bf16[128,160,128]{2,1,0:T(8,128)(2,1)S(1)} %all_to_all.16.r_ref, bf16[20,100,640]{2,1,0:T(8,128)(2,1)S(1)} %bitcast.7, bf16[640,640]{1,0:T(8,128)(2,1)S(1)} %copy-done.1), custom_call_target="tpu_custom_call" | custom-call | tf_op jit(solution)/shard_map/pallas_call | solution.py:270
  134.9 13.9 %all_to_all.17.sums_ref = f32[128,1,128]{2,1,0:T(1,128)S(1)} all-to-all(f32[128,1,128]{2,1,0:T(1,128)S(1)} %get-tuple-element.13), channel_id=1, replica_groups=mesh['act'=4,'virt_0'=4,'virt_1'=4,'core'=2] {'act','core','virt_0','vir..., dimensions={0} | all-to-all | bytes 131072 | tf_op jit(solution)/shard_map/all_to_all | solution.py:323
  148.8 2.5 %shard_map.70 = (bf16[20,100,640]{2,1,0:T(8,128)(2,1)}, f32[1,128]{1,0:T(1,128)}, f32[1,128]{1,0:T(1,128)}) custom-call(f32[128,1,128]{2,1,0:T(1,128)S(1)} %all_to_all.17.sums_ref, f32[2080,640]{1,0:T(8,128)S(1)} %get-tuple-element.14.sigma_ref, bf16[2080,640]{1,0:T(8,128)(2,1)S(1)} %get-tuple-element.15.w_ref), custom_call_target="tpu_custom_call" | custom-call | tf_op jit(solution)/shard_map/pallas_call | solution.py:312
Async XLA Ops:
  5.0 46.5 %copy-start.1 = (bf16[640,640]{1,0:T(8,128)(2,1)S(1)}, bf16[640,640]{1,0:T(8,128)(2,1)}, u32[]{:S(2)}) copy-start(bf16[640,640]{1,0:T(8,128)(2,1)} %f_ref.3) | copy-start | bytes 2457604
  59.7 68.1 %copy-start = (bf16[100,20,640]{2,0,1:T(8,128)(2,1)S(1)}, bf16[100,20,640]{2,0,1:T(8,128)(2,1)}, u32[]{:S(2)}) copy-start(bf16[100,20,640]{2,0,1:T(8,128)(2,1)} %param.4) | copy-start | bytes 7680004
